TPU v7x, 32 devices: a whole 2x2x4 slice. The times are simulated.
32 devices in a mesh: dp: 8 (over z, x), mp: 4 (over y, core).
Axes of the slice: x: 2, y: 2, z: 4, core: 2. Of those that a mesh axis runs over, the one named last changes fastest.
Arguments:
- tokens: bfloat16 [8, 196, 1280], P('dp'), may hold values from -6 to 6
- pad_mask: int32 [8, 196], P('dp'), may hold values from 0 to 1, as said below
- cotangent: bfloat16 [8, 196, 1280], P('dp'), may hold values from -6 to 6
- norm_gains: float32 [2, 1280], replicated, may hold values from 0.5 to 1.5
- norm_biases: float32 [2, 1280], replicated, may hold values from -2 to 2
- out_biases: float32 [2, 1280], replicated, may hold values from -2 to 2
- qkv_bias: float32 [3840], P('mp'), may hold values from -2 to 2
- up_bias: float32 [5120], P('mp'), may hold values from -2 to 2
- rel_pos: float32 [2, 27, 80], replicated, may hold values from -0.6 to 0.6
- attn_owner: int32 [4, 64], P('mp'), may hold values from 0 to 63, as said below
- mlp_owner: int32 [4, 128], P('mp'), may hold values from 0 to 127, as said below
- attn_master: float32 [4, 64, 25600], P('mp', 'dp')
- mlp_master: float32 [4, 128, 25600], P('mp', 'dp')
- attn_left: float32 [4, 64, 25600], P('mp', 'dp'), may hold values from -0.5 to 0.5
- attn_right: float32 [4, 64, 25600], P('mp', 'dp'), may hold values from -0.5 to 0.5
- mlp_left: float32 [4, 128, 25600], P('mp', 'dp'), may hold values from -0.5 to 0.5
- mlp_right: float32 [4, 128, 25600], P('mp', 'dp'), may hold values from -0.5 to 0.5
- attn_first: float32 [4, 64, 25600], P('mp', 'dp')
- attn_second: float32 [4, 64, 25600], P('mp', 'dp'), as said below
- mlp_first: float32 [4, 128, 25600], P('mp', 'dp')
- mlp_second: float32 [4, 128, 25600], P('mp', 'dp'), as said below
Outputs:
- block_output: bfloat16 [8, 196, 1280], P('dp')
- tokens_grad: float32 [8, 196, 1280], P('dp')
- gains_grad: float32 [2, 1280], replicated
- biases_grad: float32 [2, 1280], replicated
- out_biases_grad: float32 [2, 1280], replicated
- qkv_bias_grad: float32 [3840], P('mp')
- up_bias_grad: float32 [5120], P('mp')
- rel_pos_grad: float32 [2, 27, 80], replicated
- attn_grad: float32 [4, 64, 25600], P('mp', 'dp')
- mlp_grad: float32 [4, 128, 25600], P('mp', 'dp')
- attn_new: float32 [4, 64, 25600], P('mp', 'dp')
- mlp_new: float32 [4, 128, 25600], P('mp', 'dp')
- attn_copy: bfloat16 [4, 64, 25600], P('mp', 'dp')
- mlp_copy: bfloat16 [4, 128, 25600], P('mp', 'dp')
- attn_first_new: float32 [4, 64, 25600], P('mp', 'dp')
- attn_second_new: float32 [4, 64, 25600], P('mp', 'dp')
- mlp_first_new: float32 [4, 128, 25600], P('mp', 'dp')
- mlp_second_new: float32 [4, 128, 25600], P('mp', 'dp')
Inputs may be any that keep to these rules, and one draw needn't show every extreme that they name: `pad_mask`: slot s holds window s mod (25) of image s // 25, windows row-major in a 5 x 5 grid of 14 x 14 tokens, tokens row-major; slots of images from 1 on are all 0; in each image the 1 entries form a 64 x 64 square at an offset of 0 to 6 rows and columns. `attn_owner`: each row is a permutation of 0 to 63. `mlp_owner`: each row is a permutation of 0 to 127. `attn_second`: every entry is positive. `mlp_second`: every entry is positive.
All inputs are finite; a program needn't handle non-finite values.
Results may differ from a plain program's by a relative error of at most 0.017.
Values may be sent and summed in bfloat16 or wider, within the bound.
A program may use at most 192 MiB of HBM per device.

v0:
```python
import math
import jax
import jax.numpy as jnp
from jax import lax
from jax.sharding import PartitionSpec as P

highest = lax.Precision.HIGHEST
norm_eps = 1e-06
beta_one = 0.9
beta_two = 0.95
adam_eps = 1e-08
learn_rate = 0.02


def untile(tile_rows, row_count, col_count, tile_side):
    shaped = tile_rows.reshape(row_count // tile_side, col_count // tile_side, tile_side, tile_side)
    return shaped.transpose(0, 2, 1, 3).reshape(row_count, col_count)


def retile(matrix, tile_side):
    row_count, col_count = matrix.shape
    shaped = matrix.reshape(row_count // tile_side, tile_side, col_count // tile_side, tile_side)
    return shaped.transpose(0, 2, 1, 3).reshape(-1, tile_side * tile_side)


def rel_onehot(win_side):
    positions = jnp.arange(win_side, dtype=jnp.int32)
    offset = positions[:, None] - positions[None, :] + (win_side - 1)
    entries = jnp.arange(2 * win_side - 1, dtype=jnp.int32)
    return (offset[:, :, None] == entries[None, None, :]).astype(jnp.float32)


def norm_forward(values, norm_gain, norm_shift):
    centre = values - jnp.mean(values, axis=-1, keepdims=True)
    inverse = lax.rsqrt(jnp.mean(centre * centre, axis=-1, keepdims=True) + norm_eps)
    unit_rows = centre * inverse
    return (unit_rows * norm_gain + norm_shift, unit_rows, inverse)


def norm_backward(grad_in, unit_rows, inverse, norm_gain):
    grad_unit = grad_in * norm_gain
    centred = grad_unit - jnp.mean(grad_unit, axis=-1, keepdims=True)
    return inverse * (centred - unit_rows * jnp.mean(grad_unit * unit_rows, axis=-1, keepdims=True))


def gelu_pair(values):
    normal_cdf = 0.5 * (1.0 + lax.erf(values * 0.5**0.5))
    density = jnp.exp(-0.5 * values * values) * (2.0 * math.pi) ** (-0.5)
    return (values * normal_cdf, normal_cdf + values * density)


def soap_step(grad_tiles, master, left_basis, right_basis, first_moment, second_moment):
    tile_side = math.isqrt(grad_tiles.shape[2])
    square = (grad_tiles.shape[0], grad_tiles.shape[1], tile_side, tile_side)
    left_square = left_basis.reshape(square)
    right_square = right_basis.reshape(square)
    half_turn = jnp.einsum(
        "mtji,mtjk->mtik", left_square, grad_tiles.reshape(square), precision=highest
    )
    rotated = jnp.einsum("mtik,mtkl->mtil", half_turn, right_square, precision=highest).reshape(
        grad_tiles.shape
    )
    first_new = beta_one * first_moment + (1.0 - beta_one) * rotated
    second_new = beta_two * second_moment + (1.0 - beta_two) * rotated * rotated
    direction = (first_new / (jnp.sqrt(second_new) + adam_eps)).reshape(square)
    back_half = jnp.einsum("mtij,mtjk->mtik", left_square, direction, precision=highest)
    update = jnp.einsum("mtik,mtlk->mtil", back_half, right_square, precision=highest).reshape(
        grad_tiles.shape
    )
    master_new = master - learn_rate * update
    return (master_new, master_new.astype(jnp.bfloat16), first_new, second_new)


def local(
    tokens,
    pad_mask,
    cotangent,
    norm_gains,
    norm_biases,
    out_biases,
    qkv_bias,
    up_bias,
    rel_pos,
    attn_owner,
    mlp_owner,
    attn_master,
    mlp_master,
    attn_left,
    attn_right,
    mlp_left,
    mlp_right,
    attn_first,
    attn_second,
    mlp_first,
    mlp_second,
):
    windows, win_tokens, model_width = tokens.shape
    row_count = windows * win_tokens
    qkv_cols = qkv_bias.shape[0]
    head_cols = qkv_cols // 3
    unit_cols = up_bias.shape[0]
    head_dim = rel_pos.shape[2]
    heads_here = head_cols // head_dim
    win_side = (rel_pos.shape[1] + 1) // 2
    tile_side = math.isqrt(attn_master.shape[2])
    qkv_count = model_width // tile_side * (qkv_cols // tile_side)
    up_count = model_width // tile_side * (unit_cols // tile_side)
    score_scale = head_dim ** (-0.5)
    attn_stored, mlp_stored = (
        lax.all_gather(attn_master.astype(jnp.bfloat16), "dp", axis=1, tiled=True),
        lax.all_gather(mlp_master.astype(jnp.bfloat16), "dp", axis=1, tiled=True),
    )
    attn_order = jnp.argsort(attn_owner[0])
    mlp_order = jnp.argsort(mlp_owner[0])
    attn_sorted = attn_stored[0][attn_order]
    mlp_sorted = mlp_stored[0][mlp_order]
    w_qkv = untile(attn_sorted[:qkv_count], model_width, qkv_cols, tile_side)
    w_proj = untile(attn_sorted[qkv_count:], head_cols, model_width, tile_side)
    w_up = untile(mlp_sorted[:up_count], model_width, unit_cols, tile_side)
    w_down = untile(mlp_sorted[up_count:], unit_cols, model_width, tile_side)
    onehot = rel_onehot(win_side)
    table_h = jnp.einsum("ijr,rc->ijc", onehot, rel_pos[0], precision=highest)
    table_w = jnp.einsum("ijr,rc->ijc", onehot, rel_pos[1], precision=highest)
    flat_rows = tokens.reshape(row_count, model_width).astype(jnp.float32)
    live_rows = pad_mask.reshape(row_count, 1).astype(jnp.float32)
    normed, unit_one, inverse_one = norm_forward(flat_rows, norm_gains[0], norm_biases[0])
    normed_low = (normed * live_rows).astype(jnp.bfloat16)
    mixed_rows = (jnp.dot(normed_low, w_qkv, preferred_element_type=jnp.float32) + qkv_bias).astype(
        jnp.bfloat16
    )
    head_parts = mixed_rows.reshape(windows, win_tokens, 3, heads_here, head_dim)
    queries = head_parts[:, :, 0]
    key_rows = head_parts[:, :, 1]
    value_rows = head_parts[:, :, 2]
    query_grid = queries.astype(jnp.float32).reshape(
        windows, win_side, win_side, heads_here, head_dim
    )

    def score_rows():
        direct = (
            jnp.einsum("wqhc,wkhc->whqk", queries, key_rows, preferred_element_type=jnp.float32)
            * score_scale
        )
        along_h = jnp.einsum("wabhc,akc->whabk", query_grid, table_h, precision=highest)
        along_w = jnp.einsum("wabhc,blc->whabl", query_grid, table_w, precision=highest)
        return direct + (along_h[..., :, None] + along_w[..., None, :]).reshape(
            windows, heads_here, win_tokens, win_tokens
        )

    scores = score_rows()
    row_top = jnp.max(scores, axis=-1, keepdims=True)
    exponent = jnp.exp(scores - row_top)
    row_total = jnp.sum(exponent, axis=-1, keepdims=True)
    log_total = row_top + jnp.log(row_total)
    probs_low = (exponent / row_total).astype(jnp.bfloat16)
    attended = jnp.einsum(
        "whqk,wkhc->wqhc", probs_low, value_rows, preferred_element_type=jnp.float32
    )
    attended_low = attended.reshape(row_count, head_cols).astype(jnp.bfloat16)
    branch = lax.psum(
        jnp.dot(attended_low, w_proj, preferred_element_type=jnp.float32).astype(jnp.bfloat16), "mp"
    ).astype(jnp.float32)
    middle = flat_rows + branch + out_biases[0]
    second, unit_two, inverse_two = norm_forward(middle, norm_gains[1], norm_biases[1])
    second_low = second.astype(jnp.bfloat16)
    hidden = jnp.dot(second_low, w_up, preferred_element_type=jnp.float32) + up_bias
    active, gelu_slope = gelu_pair(hidden)
    active_low = active.astype(jnp.bfloat16)
    down_sum = lax.psum(
        jnp.dot(active_low, w_down, preferred_element_type=jnp.float32).astype(jnp.bfloat16), "mp"
    ).astype(jnp.float32)
    block_output = (
        ((middle + down_sum + out_biases[1]) * live_rows)
        .astype(jnp.bfloat16)
        .reshape(windows, win_tokens, model_width)
    )
    grad_out = cotangent.reshape(row_count, model_width).astype(jnp.float32) * live_rows
    grad_out_low = grad_out.astype(jnp.bfloat16)
    down_bias_grad = jnp.sum(grad_out, axis=0)
    w_down_grad = jnp.einsum(
        "nf,nd->fd", active_low, grad_out_low, preferred_element_type=jnp.float32
    )
    grad_active = jnp.einsum("nd,fd->nf", grad_out_low, w_down, preferred_element_type=jnp.float32)
    grad_hidden = (grad_active * gelu_slope).astype(jnp.bfloat16)
    up_bias_grad = jnp.sum(grad_hidden.astype(jnp.float32), axis=0)
    w_up_grad = jnp.einsum("nd,nf->df", second_low, grad_hidden, preferred_element_type=jnp.float32)
    mlp_stack = jnp.concatenate(
        [retile(w_up_grad, tile_side), retile(w_down_grad, tile_side)], axis=0
    )[mlp_owner[0]][None]
    grad_second = lax.psum(
        jnp.einsum("nf,df->nd", grad_hidden, w_up, preferred_element_type=jnp.float32).astype(
            jnp.bfloat16
        ),
        "mp",
    ).astype(jnp.float32)
    gain_two_grad = jnp.sum(grad_second * unit_two, axis=0)
    shift_two_grad = jnp.sum(grad_second, axis=0)
    grad_middle = grad_out + norm_backward(grad_second, unit_two, inverse_two, norm_gains[1])
    proj_bias_grad = jnp.sum(grad_middle, axis=0)
    grad_branch = grad_middle.astype(jnp.bfloat16)
    w_proj_grad = jnp.einsum(
        "nc,nd->cd", attended_low, grad_branch, preferred_element_type=jnp.float32
    )
    grad_attended = jnp.einsum("nd,cd->nc", grad_branch, w_proj, preferred_element_type=jnp.float32)
    grad_attended = grad_attended.astype(jnp.bfloat16).reshape(
        windows, win_tokens, heads_here, head_dim
    )
    probs_full = jnp.exp(score_rows() - log_total)
    probs_again = probs_full.astype(jnp.bfloat16)
    grad_probs = jnp.einsum(
        "wqhc,wkhc->whqk", grad_attended, value_rows, preferred_element_type=jnp.float32
    )
    grad_values = jnp.einsum(
        "whqk,wqhc->wkhc", probs_again, grad_attended, preferred_element_type=jnp.float32
    )
    grad_scores = (
        probs_full * (grad_probs - jnp.sum(probs_full * grad_probs, axis=-1, keepdims=True))
    ).astype(jnp.bfloat16)
    grad_queries = (
        jnp.einsum("whqk,wkhc->wqhc", grad_scores, key_rows, preferred_element_type=jnp.float32)
        * score_scale
    )
    grad_keys = (
        jnp.einsum("whqk,wqhc->wkhc", grad_scores, queries, preferred_element_type=jnp.float32)
        * score_scale
    )
    grad_grid = grad_scores.astype(jnp.float32).reshape(
        windows, heads_here, win_side, win_side, win_side, win_side
    )
    grad_h = jnp.sum(grad_grid, axis=5)
    grad_w = jnp.sum(grad_grid, axis=4)
    grad_rel_q = jnp.einsum("whabk,akc->wabhc", grad_h, table_h, precision=highest) + jnp.einsum(
        "whabl,blc->wabhc", grad_w, table_w, precision=highest
    )
    grad_queries = grad_queries + grad_rel_q.reshape(windows, win_tokens, heads_here, head_dim)
    table_h_grad = jnp.einsum("whabk,wabhc->akc", grad_h, query_grid, precision=highest)
    table_w_grad = jnp.einsum("whabl,wabhc->blc", grad_w, query_grid, precision=highest)
    rel_part = jnp.stack(
        [
            jnp.einsum("ijr,ijc->rc", onehot, table_h_grad, precision=highest),
            jnp.einsum("ijr,ijc->rc", onehot, table_w_grad, precision=highest),
        ]
    )
    grad_mixed = (
        jnp.stack([grad_queries, grad_keys, grad_values], axis=2)
        .reshape(row_count, qkv_cols)
        .astype(jnp.bfloat16)
    )
    qkv_bias_grad = jnp.sum(grad_mixed.astype(jnp.float32), axis=0)
    w_qkv_grad = jnp.einsum("nd,nc->dc", normed_low, grad_mixed, preferred_element_type=jnp.float32)
    grad_normed, rel_sum = (
        lax.psum(
            jnp.einsum("nc,dc->nd", grad_mixed, w_qkv, preferred_element_type=jnp.float32).astype(
                jnp.bfloat16
            ),
            "mp",
        ).astype(jnp.float32),
        lax.psum(rel_part.astype(jnp.bfloat16), "mp").astype(jnp.float32),
    )
    grad_normed = grad_normed * live_rows
    gain_one_grad = jnp.sum(grad_normed * unit_one, axis=0)
    shift_one_grad = jnp.sum(grad_normed, axis=0)
    tokens_grad = (
        grad_middle + norm_backward(grad_normed, unit_one, inverse_one, norm_gains[0])
    ).reshape(windows, win_tokens, model_width)
    attn_stack = jnp.concatenate(
        [retile(w_qkv_grad, tile_side), retile(w_proj_grad, tile_side)], axis=0
    )[attn_owner[0]][None]
    attn_grad, mlp_grad = (
        lax.psum_scatter(attn_stack, "dp", scatter_dimension=1, tiled=True),
        lax.psum_scatter(mlp_stack, "dp", scatter_dimension=1, tiled=True),
    )
    gains_grad, biases_grad, out_biases_grad, rel_pos_grad, qkv_bias_total, up_bias_total = (
        lax.psum(
            (
                jnp.stack([gain_one_grad, gain_two_grad]),
                jnp.stack([shift_one_grad, shift_two_grad]),
                jnp.stack([proj_bias_grad, down_bias_grad]),
                rel_sum,
                qkv_bias_grad,
                up_bias_grad,
            ),
            "dp",
        )
    )
    attn_new, attn_copy, attn_first_new, attn_second_new = soap_step(
        attn_grad, attn_master, attn_left, attn_right, attn_first, attn_second
    )
    mlp_new, mlp_copy, mlp_first_new, mlp_second_new = soap_step(
        mlp_grad, mlp_master, mlp_left, mlp_right, mlp_first, mlp_second
    )
    return (
        block_output,
        tokens_grad,
        gains_grad,
        biases_grad,
        out_biases_grad,
        qkv_bias_total,
        up_bias_total,
        rel_pos_grad,
        attn_grad,
        mlp_grad,
        attn_new,
        mlp_new,
        attn_copy,
        mlp_copy,
        attn_first_new,
        attn_second_new,
        mlp_first_new,
        mlp_second_new,
    )


def solution(mesh):
    placed = (
        P("dp", None, None),
        P("dp", None),
        P("dp", None, None),
        P(),
        P(),
        P(),
        P("mp"),
        P("mp"),
        P(),
        P("mp", None),
        P("mp", None),
        P("mp", "dp", None),
        P("mp", "dp", None),
        P("mp", "dp", None),
        P("mp", "dp", None),
        P("mp", "dp", None),
        P("mp", "dp", None),
        P("mp", "dp", None),
        P("mp", "dp", None),
        P("mp", "dp", None),
        P("mp", "dp", None),
    )
    return jax.shard_map(
        local,
        mesh=mesh,
        in_specs=placed,
        out_specs=(
            P("dp", None, None),
            P("dp", None, None),
            P(),
            P(),
            P(),
            P("mp"),
            P("mp"),
            P(),
            P("mp", "dp", None),
            P("mp", "dp", None),
            P("mp", "dp", None),
            P("mp", "dp", None),
            P("mp", "dp", None),
            P("mp", "dp", None),
            P("mp", "dp", None),
            P("mp", "dp", None),
            P("mp", "dp", None),
            P("mp", "dp", None),
        ),
        check_vma=False,
    )
```

profile of v0, /device:TPU:0, one launch (start us, length us, event | category | flops | bytes accessed | tf_op | source)
XLA Modules:
  0.0 886.3 jit_solution(16054658435756151305)
XLA Ops:
  17.7 57.3 %all-gather.3.cloned.1.call-done = bf16[1,64,25600]{2,1,0:T(8,128)(2,1)} async-done(((bf16[1,8,25600]{2,1,0:T(8,128)(2,1)}), bf16[1,64,25600]{2,1,0:T(8,128)(2,1)}) %all-gather.3.cloned.1.call-update) | async-done | bytes 3276816 | tf_op jit(solution)/shard_map/all_gather | solution.py:110
  75.0 9.5 %gather_fusion = bf16[64,25600]{1,0:T(8,128)(2,1)} fusion(bf16[64,25600]{1,0:T(8,128)(2,1)} %bitcast.343, s32[1024]{0:T(1024)S(1)} %pad_clamp_fusion.3), kind=kCustom, calls=%fused_computation | custom fusion | bytes 6553856 | tf_op jit(solution)/shard_map/gather | solution.py:115
  140.4 26.9 %all-reduce.6.cloned.1.call-done = bf16[196,1280]{1,0:T(8,128)(2,1)} async-done(((bf16[196,1280]{1,0:T(8,128)(2,1)}), bf16[196,1280]{1,0:T(8,128)(2,1)}) %all-reduce.6.cloned.1.call-update) | async-done | bytes 501776 | tf_op jit(solution)/shard_map/psum | solution.py:160
  170.0 102.3 %all-gather.5.cloned.1.call-done = bf16[1,128,25600]{2,1,0:T(8,128)(2,1)} async-done(((bf16[1,16,25600]{2,1,0:T(8,128)(2,1)}), bf16[1,128,25600]{2,1,0:T(8,128)(2,1)}) %all-gather.5.cloned.1.call-update) | async-done | bytes 6553616 | tf_op jit(solution)/shard_map/all_gather | solution.py:111
  272.2 17.0 %gather_fusion.1 = bf16[128,25600]{1,0:T(8,128)(2,1)} fusion(bf16[128,25600]{1,0:T(8,128)(2,1)} %bitcast.342, s32[1024]{0:T(1024)S(1)} %pad_clamp_fusion.2), kind=kCustom, calls=%fused_computation.1 | custom fusion | bytes 13107712 | tf_op jit(solution)/shard_map/gather | solution.py:116
  295.3 9.7 %reshape.655 = bf16[8,8,160,160]{3,2,1,0:T(8,128)(2,1)} reshape(bf16[64,25600]{1,0:T(8,128)(2,1)} %get-tuple-element.115) | data formatting | bytes 6553600 | tf_op jit(solution)/shard_map/reshape | solution.py:16
  305.0 8.0 copy.177
  313.0 9.2 %reshape.656 = bf16[1280,1280]{1,0:T(8,128)(2,1)} reshape(bf16[8,160,8,160]{3,2,1,0:T(8,128)(2,1)} %bitcast.347) | data formatting | bytes 6553600 | tf_op jit(solution)/shard_map/reshape | solution.py:17
  322.2 9.7 %reshape.657 = bf16[8,8,160,160]{3,2,1,0:T(8,128)(2,1)} reshape(bf16[64,25600]{1,0:T(8,128)(2,1)} %get-tuple-element.116) | data formatting | bytes 6553600 | tf_op jit(solution)/shard_map/reshape | solution.py:16
  339.8 9.6 %reshape.658 = bf16[1280,1280]{1,0:T(8,128)(2,1)} reshape(bf16[8,160,8,160]{3,2,1,0:T(8,128)(2,1)} %bitcast.348) | data formatting | bytes 6553600 | tf_op jit(solution)/shard_map/reshape | solution.py:17
  362.2 27.6 %all-reduce.8.cloned.1.call-done = bf16[196,1280]{1,0:T(8,128)(2,1)} async-done(((bf16[196,1280]{1,0:T(8,128)(2,1)}), bf16[196,1280]{1,0:T(8,128)(2,1)}) %all-reduce.8.cloned.1.call-update) | async-done | bytes 501776 | tf_op jit(solution)/shard_map/psum | solution.py:190
  430.9 27.0 %all-reduce.10.cloned.1.call-done = (bf16[196,1280]{1,0:T(8,128)(2,1)}, bf16[196,1280]{1,0:T(8,128)(2,1)}) async-done(((bf16[196,1280]{1,0:T(8,128)(2,1)}, bf16[196,1280]{1,0:T(8,128)(2,1)}), (bf16[196,1280]{1,0:T(8,128)(2,1)}, bf16[196,1280]{1,0:T(8,128)(2,1)})) %all-reduce.10.cloned.1.call-update) | async-done | bytes 1003536 | tf_op jit(solution)/shard_map/psum | solution.py:169
  468.3 9.4 %reshape.665 = f32[48,25600]{1,0:T(8,128)} reshape(f32[8,6,160,160]{3,2,1,0:T(8,128)} %convolution_bitcast_fusion.1) | data formatting | bytes 9830400 | tf_op jit(solution)/shard_map/reshape | solution.py:23
  483.3 10.7 %gather_fusion.2 = f32[64,25600]{1,0:T(8,128)} fusion(f32[64,25600]{1,0:T(8,128)} %pad_maximum_fusion.1, s32[1024]{0:T(1024)S(1)} %pad_clamp_fusion.1), kind=kCustom, calls=%fused_computation.2 | custom fusion | bytes 13107456 | tf_op jit(solution)/shard_map/gather | solution.py:266
  499.5 11.1 %reshape.667 = f32[8,160,8,160]{3,2,1,0:T(8,128)} reshape(f32[1280,1280]{1,0:T(8,128)} %fusion.96) | data formatting | bytes 13107200 | tf_op jit(solution)/shard_map/reshape | solution.py:22
  510.6 11.2 %copy.122 = f32[8,8,160,160]{3,2,1,0:T(8,128)} copy(f32[8,8,160,160]{3,1,2,0:T(8,128)} %bitcast.345) | data formatting | bytes 13107200 | tf_op jit(solution)/shard_map/transpose | solution.py:23
  521.7 12.1 %reshape.668 = f32[64,25600]{1,0:T(8,128)} reshape(f32[8,8,160,160]{3,2,1,0:T(8,128)} %copy.122) | data formatting | bytes 13107200 | tf_op jit(solution)/shard_map/reshape | solution.py:23
  539.5 12.0 %reshape.669 = f32[64,25600]{1,0:T(8,128)} reshape(f32[8,8,160,160]{3,2,1,0:T(8,128)} %convolution_bitcast_fusion) | data formatting | bytes 13107200 | tf_op jit(solution)/shard_map/reshape | solution.py:23
  551.6 11.0 %pad_maximum_fusion = f32[128,25600]{1,0:T(8,128)} fusion(f32[64,25600]{1,0:T(8,128)} %reshape.669, f32[64,25600]{1,0:T(8,128)} %reshape.668), kind=kLoop, calls=%fused_computation.4 | loop fusion | flops 3276800 | bytes 26214400 | tf_op jit(solution)/shard_map/concatenate | solution.py:187
  562.6 19.3 %gather_fusion.3 = f32[128,25600]{1,0:T(8,128)} fusion(f32[128,25600]{1,0:T(8,128)} %pad_maximum_fusion, s32[1024]{0:T(1024)S(1)} %pad_clamp_fusion), kind=kCustom, calls=%fused_computation.3 | custom fusion | bytes 26214912 | tf_op jit(solution)/shard_map/gather | solution.py:187
  595.0 11.3 %psum.86 = bf16[2,27,80]{2,1,0:T(8,128)(2,1)S(1)} all-reduce(bf16[2,27,80]{2,1,0:T(8,128)(2,1)S(1)} %pad_maximum_fusion.2), channel_id=1, replica_groups=mesh['dp'=8,'mp'=4] {'mp'}, use_global_device_ids=true, to_apply=%region_32.33 | all-reduce | flops 4320 | bytes 17280 | tf_op jit(solution)/shard_map/psum | solution.py:258
  609.6 40.8 %all-reduce = (f32[2,1280]{1,0:T(2,128)}, f32[2,1280]{1,0:T(2,128)}, f32[2,1280]{1,0:T(2,128)}, f32[960]{0:T(1024)}, f32[1280]{0:T(1024)}, /*index=5*/f32[2,27,80]{2,1,0:T(8,128)S(1)}) all-reduce(f32[2,1280]{1,0:T(2,128)S(1)} %pad_maximum_fusion.3, f32[2,1280]{1,0:T(2,128)S(1)} %pad_maximum_fusion.4, ...), channel_id=1, replica_groups=mesh['dp'=8,'mp'=4] {'dp'}, use_global_device_ids=true, to_apply=%region_21.22 | all-reduce | flops 14240 | bytes 105280 | tf_op jit(solution)/shard_map/psum | solution.py:274
  680.3 154.9 %reduce-scatter.5.cloned.1.call-done = f32[1,16,25600]{2,1,0:T(8,128)} async-done(((f32[1,128,25600]{2,1,0:T(8,128)}), f32[1,16,25600]{2,1,0:T(8,128)}) %reduce-scatter.5.cloned.1.call-update) | async-done | bytes 1638416 | tf_op jit(solution)/shard_map/reduce_scatter | solution.py:271
  839.1 8.1 fusion.111
  (247 shorter events, 245.3 us)
Async XLA Ops:
  7.2 10.2 %copy-start = (bf16[1,196,1280]{2,1,0:T(8,128)(2,1)S(1)}, bf16[1,196,1280]{2,1,0:T(8,128)(2,1)}, u32[]{:S(2)}) copy-start(bf16[1,196,1280]{2,1,0:T(8,128)(2,1)} %param.21) | copy-start | bytes 1505284
  7.2 67.8 %all-gather.3.cloned.1.call-start = ((), (), s32[]{:S(2)}) async-start(), calls=%async_computation.2 | async-start | bytes 3686400 | tf_op jit(solution)/shard_map/all_gather | solution.py:110
  9.3 158.1 %all-reduce.6.cloned.1.call-start = ((), (), s32[]{:S(2)}) async-start(), calls=%async_computation.3 | async-start | bytes 1024000 | tf_op jit(solution)/shard_map/psum | solution.py:160
  10.0 381.5 %copy-start.37 = (f32[1,196]{1,0:T(1,128)}, f32[1,196]{1,0:T(1,128)S(1)}, u32[]{:S(2)}) copy-start(f32[1,196]{1,0:T(1,128)S(1)} %convert_element_type.176) | copy-start | bytes 2356
  17.4 88.4 %copy-start.35 = (f32[196]{0:T(256)}, f32[196]{0:T(256)S(1)}, u32[]{:S(2)}) copy-start(f32[196]{0:T(256)S(1)} %broadcast_multiply_fusion.5) | copy-start | bytes 2356
  17.7 88.1 %copy-start.40 = (f32[196]{0:T(256)}, f32[196]{0:T(256)S(1)}, u32[]{:S(2)}) copy-start(f32[196]{0:T(256)S(1)} %add_rsqrt_fusion.1) | copy-start | bytes 2356
  108.8 288.4 %copy-start.15 = (bf16[196,960]{0,1:T(8,128)(2,1)}, bf16[196,960]{0,1:T(8,128)(2,1)S(1)}, u32[]{:S(2)}) copy-start(bf16[196,960]{0,1:T(8,128)(2,1)S(1)} %copy.93) | copy-start | bytes 1128964
  109.0 10.2 %copy-start.11 = (bf16[1,196,1,4,80]{4,3,1,2,0:T(4,128)(2,1)}, bf16[1,196,1,4,80]{4,3,1,2,0:T(4,128)(2,1)S(1)}, u32[]{:S(2)}) copy-start(bf16[1,196,1,4,80]{4,3,1,2,0:T(4,128)(2,1)S(1)} %copy.95) | copy-start | bytes 376324
  135.1 137.2 %all-gather.5.cloned.1.call-start = ((), (), s32[]{:S(2)}) async-start(), calls=%async_computation.4 | async-start | bytes 7372800 | tf_op jit(solution)/shard_map/all_gather | solution.py:111
  137.6 252.3 %all-reduce.8.cloned.1.call-start = ((), (), s32[]{:S(2)}) async-start(), calls=%async_computation.5 | async-start | bytes 1024000 | tf_op jit(solution)/shard_map/psum | solution.py:190
  339.8 9.6 %copy-start.1 = (bf16[196,1280]{1,0:T(8,128)(2,1)S(1)}, bf16[196,1280]{1,0:T(8,128)(2,1)}, u32[]{:S(2)}) copy-start(bf16[196,1280]{1,0:T(8,128)(2,1)} %all-reduce.6.cloned.1.call-done) | copy-start | bytes 1505284
  339.8 9.6 %copy-start.43 = (f32[1280]{0:T(1024)S(1)}, f32[1280]{0:T(1024)}, u32[]{:S(2)}) copy-start(f32[1280]{0:T(1024)} %param.28) | copy-start | bytes 15364
  358.2 99.7 %all-reduce.10.cloned.1.call-start = ((), (), s32[]{:S(2)}) async-start(), calls=%async_computation.8 | async-start | bytes 2048000 | tf_op jit(solution)/shard_map/psum | solution.py:169
  411.0 8.8 copy-start.5
  421.4 229.6 %reduce-scatter.3.cloned.1.call-start = ((), (), s32[]{:S(2)}) async-start(), calls=%async_computation.6 | async-start | bytes 7372800 | tf_op jit(solution)/shard_map/reduce_scatter | solution.py:270
  426.3 31.6 %copy-start.23 = (bf16[1,196,1280]{2,1,0:T(8,128)(2,1)S(1)}, bf16[1,196,1280]{2,1,0:T(8,128)(2,1)}, u32[]{:S(2)}) copy-start(bf16[1,196,1280]{2,1,0:T(8,128)(2,1)} %param.23) | copy-start | bytes 1505284
  426.3 31.6 %copy-start.36 = (f32[196]{0:T(256)S(1)}, f32[196]{0:T(256)}, u32[]{:S(2)}) copy-start(f32[196]{0:T(256)} %copy-done.35) | copy-start | bytes 2356
  426.3 31.6 %copy-start.38 = (f32[1,196]{1,0:T(1,128)S(1)}, f32[1,196]{1,0:T(1,128)}, u32[]{:S(2)}) copy-start(f32[1,196]{1,0:T(1,128)} %copy-done.37) | copy-start | bytes 2356
  426.3 31.6 %copy-start.41 = (f32[196]{0:T(256)S(1)}, f32[196]{0:T(256)}, u32[]{:S(2)}) copy-start(f32[196]{0:T(256)} %copy-done.40) | copy-start | bytes 2356
  426.3 34.0 %copy-start.7 = (f32[196,1280]{1,0:T(8,128)S(1)}, f32[196,1280]{1,0:T(8,128)}, u32[]{:S(2)}) copy-start(f32[196,1280]{1,0:T(8,128)} %copy-done.6) | copy-start | bytes 3010564
  468.3 9.4 %copy-start.8 = (f32[16,25600]{1,0:T(8,128)S(1)}, f32[16,25600]{1,0:T(8,128)}, u32[]{:S(2)}) copy-start(f32[16,25600]{1,0:T(8,128)} %reshape.666) | copy-start | bytes 4915204
  494.1 341.1 %reduce-scatter.5.cloned.1.call-start = ((), (), s32[]{:S(2)}) async-start(), calls=%async_computation.7 | async-start | bytes 14745600 | tf_op jit(solution)/shard_map/reduce_scatter | solution.py:271
  521.7 12.2 %copy-start.21 = (bf16[1280,196]{0,1:T(8,128)(2,1)S(1)}, bf16[1280,196]{0,1:T(8,128)(2,1)}, u32[]{:S(2)}) copy-start(bf16[1280,196]{0,1:T(8,128)(2,1)} %get-tuple-element.121) | copy-start | bytes 1505284
  591.9 17.6 %copy-start.42 = (f32[1280]{0:T(1024)S(1)}, f32[1280]{0:T(1024)}, u32[]{:S(2)}) copy-start(f32[1280]{0:T(1024)} %get-tuple-element.128) | copy-start | bytes 15364
  (33 other events, 108.7 us)
Sparse Core Ops, SparseCore 0:
  10.8 64.1 all-gather.2
  135.2 32.0 all-reduce.5
  170.1 102.1 all-gather.4
  358.3 31.4 all-reduce.7
  421.5 36.3 all-reduce.9
  494.2 122.6 reduce-scatter.2
  621.1 214.0 reduce-scatter.4
where the time goes:
time: 895 us; the launch traced here: 886 us
  waiting for transfers between devices  396 us (44%)
  local copies, waits for them, and re-layouts  271 us (30%)
  matrix products  85.6 us (10%)
  other arithmetic  65.3 us (7%)
  blocking collectives  52.1 us (6%)
  between operations  15.3 us (2%)
    reduce_scatter x1, waiting for transfers between devices, local(): lax.psum_scatter(mlp_stack, 'dp', scatter_dimension=1, tiled=True)  155 us
    all_gather x1, waiting for transfers between devices, local(): lax.all_gather(mlp_master.astype(jnp.bfloat16), 'dp', axis=1, tiled=True)  102 us
    all_gather x1, waiting for transfers between devices, local(): lax.all_gather(attn_master.astype(jnp.bfloat16), 'dp', axis=1, tiled=True)  57.3 us
    reshape x8, local copies, waits for them, and re-layouts, untile(): tile_rows.reshape(row_count // tile_side, col_count // tile_side, tile_si...  54.3 us
    psum x1, blocking collectives, local(): lax.psum((jnp.stack([gain_one_grad, gain_two_grad]), jnp.stack([shift_one...  40.8 us
    reshape x4, local copies, waits for them, and re-layouts, retile(): return shaped.transpose(0, 2, 1, 3).reshape(-1, tile_side * tile_side)  38.1 us
    psum x1, waiting for transfers between devices, local(): lax.psum(jnp.einsum('nf,df->nd', grad_hidden, w_up, preferred_element_typ...  27.6 us
    reshape x4, local copies, waits for them, and re-layouts, untile(): return shaped.transpose(0, 2, 1, 3).reshape(row_count, col_count)  27.4 us
  transfers between devices with their start and end apart: 7, of which 6 were waited for; matrix products, arithmetic and copies ran while one was open for 18% of the time, Pallas kernels for 0%

commit v1 on v0

--- a/solution.py
+++ b/solution.py
@@ -10,6 +10,27 @@
 beta_two = 0.95
 adam_eps = 1e-08
 learn_rate = 0.02
+
+
+def collect(value, axis, dim):
+    size, position, span = (lax.axis_size(axis), lax.axis_index(axis), value.shape[dim])
+    right = [(i, (i + 1) % size) for i in range(size)]
+    backward = [(i, (i - 1) % size) for i in range(size)]
+    result = jnp.zeros((*value.shape[:dim], size * span, *value.shape[dim + 1 :]), value.dtype)
+    result = lax.dynamic_update_slice_in_dim(result, value, position * span, axis=dim)
+    from_left = from_right = value
+    half = size // 2
+    for step in range(1, half + 1):
+        from_left = lax.ppermute(from_left, axis, right)
+        result = lax.dynamic_update_slice_in_dim(
+            result, from_left, (position - step) % size * span, axis=dim
+        )
+        if step < size - half:
+            from_right = lax.ppermute(from_right, axis, backward)
+            result = lax.dynamic_update_slice_in_dim(
+                result, from_right, (position + step) % size * span, axis=dim
+            )
+    return result
 
 
 def untile(tile_rows, row_count, col_count, tile_side):
@@ -107,7 +128,7 @@
     up_count = model_width // tile_side * (unit_cols // tile_side)
     score_scale = head_dim ** (-0.5)
     attn_stored, mlp_stored = (
-        lax.all_gather(attn_master.astype(jnp.bfloat16), "dp", axis=1, tiled=True),
+        collect(attn_master.astype(jnp.bfloat16), "dp", 1),
         lax.all_gather(mlp_master.astype(jnp.bfloat16), "dp", axis=1, tiled=True),
     )
     attn_order = jnp.argsort(attn_owner[0])

time: 895 us -> 861 us (0.962)
  waiting for transfers between devices: 396 us -> 348 us
  starting transfers between devices: 0.46 us -> 19.9 us
    all_gather x1 -> x0, waiting for transfers between devices: 57.3 us -> none  [local(): lax.all_gather(attn_master.astype(jnp.bfloat16), 'dp', axis=1, tiled=True)]
    ppermute x0 -> x7, waiting for transfers between devices: none -> 42.8 us  [the longest x4 42.8 us: collect(): from_left = lax.ppermute(from_left, axis, right)]
    all_gather x1, waiting for transfers between devices: 102 us -> 68.8 us  [local(): lax.all_gather(mlp_master.astype(jnp.bfloat16), 'dp', axis=1, tiled=True)]
    ppermute x0 -> x7, starting transfers between devices: none -> 19.4 us  [the longest x4 10.3 us: collect(): from_left = lax.ppermute(from_left, axis, right)]
  transfers between devices with their start and end apart: 7 -> 13, of which waited for: 6 -> 9; matrix products, arithmetic and copies ran while one was open for 18% -> 19% of each run, Pallas kernels for 0% -> 0%
where the time goes in v1:
time: 861 us; the launch traced here: 854 us
  waiting for transfers between devices  348 us (40%)
  local copies, waits for them, and re-layouts  268 us (31%)
  matrix products  85.6 us (10%)
  other arithmetic  63.9 us (7%)
  blocking collectives  52 us (6%)
  starting transfers between devices  19.9 us (2%)
  between operations  16.9 us (2%)
    reduce_scatter x1, waiting for transfers between devices, local(): lax.psum_scatter(mlp_stack, 'dp', scatter_dimension=1, tiled=True)  155 us
    all_gather x1, waiting for transfers between devices, local(): lax.all_gather(mlp_master.astype(jnp.bfloat16), 'dp', axis=1, tiled=True)  68.8 us
    reshape x8, local copies, waits for them, and re-layouts, untile(): tile_rows.reshape(row_count // tile_side, col_count // tile_side, tile_si...  54.3 us
    ppermute x4, waiting for transfers between devices, collect(): from_left = lax.ppermute(from_left, axis, right)  42.8 us
    psum x1, blocking collectives, local(): lax.psum((jnp.stack([gain_one_grad, gain_two_grad]), jnp.stack([shift_one...  40.7 us
    reshape x4, local copies, waits for them, and re-layouts, retile(): return shaped.transpose(0, 2, 1, 3).reshape(-1, tile_side * tile_side)  38.1 us
    psum x1, waiting for transfers between devices, local(): lax.psum(jnp.einsum('nf,df->nd', grad_hidden, w_up, preferred_element_typ...  27.6 us
    reshape x4, local copies, waits for them, and re-layouts, untile(): return shaped.transpose(0, 2, 1, 3).reshape(row_count, col_count)  27.5 us
  transfers between devices with their start and end apart: 13, of which 9 were waited for; matrix products, arithmetic and copies ran while one was open for 19% of the time, Pallas kernels for 0%

profile of v1, /device:TPU:0, one launch (start us, length us, event | category | flops | bytes accessed | tf_op | source)
XLA Modules:
  0.0 854.0 jit_solution(16467154687473142844)
XLA Ops:
  38.4 11.8 %collective-permute-done.2 = bf16[1,8,25600]{2,1,0:T(8,128)(2,1)S(1)} collective-permute-done((bf16[1,8,25600]{2,1,0:T(8,128)(2,1)}, bf16[1,8,25600]{2,1,0:T(8,128)(2,1)S(1)}, u32[]{:S(2)}, u32[]{:S(2)}) %collective-permute-start.2) | collective-permute-done | bytes 409632 | tf_op jit(solution)/shard_map/ppermute | solution.py:24
  55.8 12.8 %collective-permute-done.4 = bf16[1,8,25600]{2,1,0:T(8,128)(2,1)S(1)} collective-permute-done((bf16[1,8,25600]{2,1,0:T(8,128)(2,1)S(1)}, bf16[1,8,25600]{2,1,0:T(8,128)(2,1)S(1)}, u32[]{:S(2)}, u32[]{:S(2)}) %collective-permute-start.4) | collective-permute-done | bytes 409632 | tf_op jit(solution)/shard_map/ppermute | solution.py:24
  71.2 10.0 %collective-permute-done.6 = bf16[1,8,25600]{2,1,0:T(8,128)(2,1)S(1)} collective-permute-done((bf16[1,8,25600]{2,1,0:T(8,128)(2,1)S(1)}, bf16[1,8,25600]{2,1,0:T(8,128)(2,1)S(1)}, u32[]{:S(2)}, u32[]{:S(2)}) %collective-permute-start.6) | collective-permute-done | bytes 409632 | tf_op jit(solution)/shard_map/ppermute | solution.py:24
  141.7 26.7 %all-reduce.6.cloned.1.call-done = bf16[196,1280]{1,0:T(8,128)(2,1)} async-done(((bf16[196,1280]{1,0:T(8,128)(2,1)}), bf16[196,1280]{1,0:T(8,128)(2,1)}) %all-reduce.6.cloned.1.call-update) | async-done | bytes 501776 | tf_op jit(solution)/shard_map/psum | solution.py:181
  171.0 68.8 %all-gather.2.cloned.1.call-done = bf16[1,128,25600]{2,1,0:T(8,128)(2,1)} async-done(((bf16[1,16,25600]{2,1,0:T(8,128)(2,1)}), bf16[1,128,25600]{2,1,0:T(8,128)(2,1)}) %all-gather.2.cloned.1.call-update) | async-done | bytes 6553616 | tf_op jit(solution)/shard_map/all_gather | solution.py:132
  239.8 17.0 %gather_fusion.1 = bf16[128,25600]{1,0:T(8,128)(2,1)} fusion(bf16[128,25600]{1,0:T(8,128)(2,1)} %bitcast.357, s32[1024]{0:T(1024)S(1)} %pad_clamp_fusion.2), kind=kCustom, calls=%fused_computation.1 | custom fusion | bytes 13107712 | tf_op jit(solution)/shard_map/gather | solution.py:137
  262.9 9.7 %reshape.671 = bf16[8,8,160,160]{3,2,1,0:T(8,128)(2,1)} reshape(bf16[64,25600]{1,0:T(8,128)(2,1)} %get-tuple-element.117) | data formatting | bytes 6553600 | tf_op jit(solution)/shard_map/reshape | solution.py:37
  280.6 9.2 %reshape.672 = bf16[1280,1280]{1,0:T(8,128)(2,1)} reshape(bf16[8,160,8,160]{3,2,1,0:T(8,128)(2,1)} %bitcast.361) | data formatting | bytes 6553600 | tf_op jit(solution)/shard_map/reshape | solution.py:38
  289.8 9.7 %reshape.673 = bf16[8,8,160,160]{3,2,1,0:T(8,128)(2,1)} reshape(bf16[64,25600]{1,0:T(8,128)(2,1)} %get-tuple-element.118) | data formatting | bytes 6553600 | tf_op jit(solution)/shard_map/reshape | solution.py:37
  307.4 9.6 %reshape.674 = bf16[1280,1280]{1,0:T(8,128)(2,1)} reshape(bf16[8,160,8,160]{3,2,1,0:T(8,128)(2,1)} %bitcast.362) | data formatting | bytes 6553600 | tf_op jit(solution)/shard_map/reshape | solution.py:38
  329.8 27.6 %all-reduce.8.cloned.1.call-done = bf16[196,1280]{1,0:T(8,128)(2,1)} async-done(((bf16[196,1280]{1,0:T(8,128)(2,1)}), bf16[196,1280]{1,0:T(8,128)(2,1)}) %all-reduce.8.cloned.1.call-update) | async-done | bytes 501776 | tf_op jit(solution)/shard_map/psum | solution.py:211
  398.4 27.0 %all-reduce.10.cloned.1.call-done = (bf16[196,1280]{1,0:T(8,128)(2,1)}, bf16[196,1280]{1,0:T(8,128)(2,1)}) async-done(((bf16[196,1280]{1,0:T(8,128)(2,1)}, bf16[196,1280]{1,0:T(8,128)(2,1)}), (bf16[196,1280]{1,0:T(8,128)(2,1)}, bf16[196,1280]{1,0:T(8,128)(2,1)})) %all-reduce.10.cloned.1.call-update) | async-done | bytes 1003536 | tf_op jit(solution)/shard_map/psum | solution.py:190
  435.8 9.4 %reshape.681 = f32[48,25600]{1,0:T(8,128)} reshape(f32[8,6,160,160]{3,2,1,0:T(8,128)} %convolution_bitcast_fusion.1) | data formatting | bytes 9830400 | tf_op jit(solution)/shard_map/reshape | solution.py:44
  450.8 10.7 %gather_fusion.2 = f32[64,25600]{1,0:T(8,128)} fusion(f32[64,25600]{1,0:T(8,128)} %pad_maximum_fusion.1, s32[1024]{0:T(1024)S(1)} %pad_clamp_fusion.1), kind=kCustom, calls=%fused_computation.2 | custom fusion | bytes 13107456 | tf_op jit(solution)/shard_map/gather | solution.py:287
  467.0 11.1 %reshape.683 = f32[8,160,8,160]{3,2,1,0:T(8,128)} reshape(f32[1280,1280]{1,0:T(8,128)} %fusion.96) | data formatting | bytes 13107200 | tf_op jit(solution)/shard_map/reshape | solution.py:43
  478.1 11.2 %copy.122 = f32[8,8,160,160]{3,2,1,0:T(8,128)} copy(f32[8,8,160,160]{3,1,2,0:T(8,128)} %bitcast.359) | data formatting | bytes 13107200 | tf_op jit(solution)/shard_map/transpose | solution.py:44
  489.3 12.1 %reshape.684 = f32[64,25600]{1,0:T(8,128)} reshape(f32[8,8,160,160]{3,2,1,0:T(8,128)} %copy.122) | data formatting | bytes 13107200 | tf_op jit(solution)/shard_map/reshape | solution.py:44
  507.1 12.0 %reshape.685 = f32[64,25600]{1,0:T(8,128)} reshape(f32[8,8,160,160]{3,2,1,0:T(8,128)} %convolution_bitcast_fusion) | data formatting | bytes 13107200 | tf_op jit(solution)/shard_map/reshape | solution.py:44
  519.1 11.0 %pad_maximum_fusion = f32[128,25600]{1,0:T(8,128)} fusion(f32[64,25600]{1,0:T(8,128)} %reshape.685, f32[64,25600]{1,0:T(8,128)} %reshape.684), kind=kLoop, calls=%fused_computation.4 | loop fusion | flops 3276800 | bytes 26214400 | tf_op jit(solution)/shard_map/concatenate | solution.py:208
  530.1 19.3 %gather_fusion.3 = f32[128,25600]{1,0:T(8,128)} fusion(f32[128,25600]{1,0:T(8,128)} %pad_maximum_fusion, s32[1024]{0:T(1024)S(1)} %pad_clamp_fusion), kind=kCustom, calls=%fused_computation.3 | custom fusion | bytes 26214912 | tf_op jit(solution)/shard_map/gather | solution.py:208
  562.5 11.3 %psum.86 = bf16[2,27,80]{2,1,0:T(8,128)(2,1)S(1)} all-reduce(bf16[2,27,80]{2,1,0:T(8,128)(2,1)S(1)} %pad_maximum_fusion.2), channel_id=1, replica_groups=mesh['dp'=8,'mp'=4] {'mp'}, use_global_device_ids=true, to_apply=%region_32.33 | all-reduce | flops 4320 | bytes 17280 | tf_op jit(solution)/shard_map/psum | solution.py:279
  577.1 40.7 %all-reduce = (f32[2,1280]{1,0:T(2,128)}, f32[2,1280]{1,0:T(2,128)}, f32[2,1280]{1,0:T(2,128)}, f32[960]{0:T(1024)}, f32[1280]{0:T(1024)}, /*index=5*/f32[2,27,80]{2,1,0:T(8,128)S(1)}) all-reduce(f32[2,1280]{1,0:T(2,128)S(1)} %pad_maximum_fusion.3, f32[2,1280]{1,0:T(2,128)S(1)} %pad_maximum_fusion.4, ...), channel_id=1, replica_groups=mesh['dp'=8,'mp'=4] {'dp'}, use_global_device_ids=true, to_apply=%region_21.22 | all-reduce | flops 14240 | bytes 105280 | tf_op jit(solution)/shard_map/psum | solution.py:295
  647.8 154.6 %reduce-scatter.5.cloned.1.call-done = f32[1,16,25600]{2,1,0:T(8,128)} async-done(((f32[1,128,25600]{2,1,0:T(8,128)}), f32[1,16,25600]{2,1,0:T(8,128)}) %reduce-scatter.5.cloned.1.call-update) | async-done | bytes 1638416 | tf_op jit(solution)/shard_map/reduce_scatter | solution.py:292
  806.3 8.1 fusion.111
  (278 shorter events, 285.4 us)
Async XLA Ops:
  8.0 160.3 %all-reduce.6.cloned.1.call-start = ((), (), s32[]{:S(2)}) async-start(), calls=%async_computation.2 | async-start | bytes 1024000 | tf_op jit(solution)/shard_map/psum | solution.py:181
  10.0 20.8 %collective-permute-start = (bf16[1,8,25600]{2,1,0:T(8,128)(2,1)}, bf16[1,8,25600]{2,1,0:T(8,128)(2,1)}, u32[]{:S(2)}, u32[]{:S(2)}) collective-permute-start(bf16[1,8,25600]{2,1,0:T(8,128)(2,1)} %get-tuple-element.116), channel_id=1, source_target_pairs={{0,4},{4,8},{8,12},{12,16},{16,20},{20,24},{24,28},{28,0},{1,5},{5... | collective-permute-start | bytes 1228808 | tf_op jit(solution)/shard_map/ppermute | solution.py:24
  13.0 20.3 %collective-permute-start.1 = (bf16[1,8,25600]{2,1,0:T(8,128)(2,1)}, bf16[1,8,25600]{2,1,0:T(8,128)(2,1)}, u32[]{:S(2)}, u32[]{:S(2)}) collective-permute-start(bf16[1,8,25600]{2,1,0:T(8,128)(2,1)} %get-tuple-element.116), channel_id=1, source_target_pairs={{0,28},{4,0},{8,4},{12,8},{16,12},{20,16},{24,20},{28,24},{1,29},{... | collective-permute-start | bytes 1228808 | tf_op jit(solution)/shard_map/ppermute | solution.py:29
  16.1 55.0 %copy-start.33 = (s32[14,14]{1,0:T(8,128)}, s32[14,14]{1,0:T(8,128)S(1)}, u32[]{:S(2)}) copy-start(s32[14,14]{1,0:T(8,128)S(1)} %subtract_add_fusion) | copy-start | bytes 2356
  19.4 87.6 %copy-start.37 = (f32[196]{0:T(256)}, f32[196]{0:T(256)S(1)}, u32[]{:S(2)}) copy-start(f32[196]{0:T(256)S(1)} %broadcast_multiply_fusion.5) | copy-start | bytes 2356
  21.3 337.8 %copy-start.39 = (f32[1,196]{1,0:T(1,128)}, f32[1,196]{1,0:T(1,128)S(1)}, u32[]{:S(2)}) copy-start(f32[1,196]{1,0:T(1,128)S(1)} %convert_element_type.176) | copy-start | bytes 2356
  22.7 84.3 %copy-start.44 = (f32[196]{0:T(256)}, f32[196]{0:T(256)S(1)}, u32[]{:S(2)}) copy-start(f32[196]{0:T(256)S(1)} %add_rsqrt_fusion.1) | copy-start | bytes 2356
  30.8 19.4 %collective-permute-start.2 = (bf16[1,8,25600]{2,1,0:T(8,128)(2,1)}, bf16[1,8,25600]{2,1,0:T(8,128)(2,1)S(1)}, u32[]{:S(2)}, u32[]{:S(2)}) collective-permute-start(bf16[1,8,25600]{2,1,0:T(8,128)(2,1)} %collective-permute-done), channel_id=1, source_target_pairs={{0,4},{4,8},{8,12},{12,16},{16,20},{20,24},{24,28},{28,0},{1,5},{5... | collective-permute-start | bytes 1228808 | tf_op jit(solution)/shard_map/ppermute | solution.py:24
  33.3 19.3 %collective-permute-start.3 = (bf16[1,8,25600]{2,1,0:T(8,128)(2,1)}, bf16[1,8,25600]{2,1,0:T(8,128)(2,1)S(1)}, u32[]{:S(2)}, u32[]{:S(2)}) collective-permute-start(bf16[1,8,25600]{2,1,0:T(8,128)(2,1)} %collective-permute-done.1), channel_id=1, source_target_pairs={{0,28},{4,0},{8,4},{12,8},{16,12},{20,16},{24,20},{28,24},{1,29},{... | collective-permute-start | bytes 1228808 | tf_op jit(solution)/shard_map/ppermute | solution.py:29
  50.3 18.3 %collective-permute-start.4 = (bf16[1,8,25600]{2,1,0:T(8,128)(2,1)S(1)}, bf16[1,8,25600]{2,1,0:T(8,128)(2,1)S(1)}, u32[]{:S(2)}, u32[]{:S(2)}) collective-permute-start(bf16[1,8,25600]{2,1,0:T(8,128)(2,1)S(1)} %collective-permute-done.2), channel_id=1, source_target_pairs={{0,4},{4,8},{8,12},{12,16},{16,20},{20,24},{24,28},{28,0},{1,5},{5... | collective-permute-start | bytes 1228808 | tf_op jit(solution)/shard_map/ppermute | solution.py:24
  52.7 18.5 %collective-permute-start.5 = (bf16[1,8,25600]{2,1,0:T(8,128)(2,1)S(1)}, bf16[1,8,25600]{2,1,0:T(8,128)(2,1)S(1)}, u32[]{:S(2)}, u32[]{:S(2)}) collective-permute-start(bf16[1,8,25600]{2,1,0:T(8,128)(2,1)S(1)} %collective-permute-done.3), channel_id=1, source_target_pairs={{0,28},{4,0},{8,4},{12,8},{16,12},{20,16},{24,20},{28,24},{1,29},{... | collective-permute-start | bytes 1228808 | tf_op jit(solution)/shard_map/ppermute | solution.py:29
  68.6 12.6 %collective-permute-start.6 = (bf16[1,8,25600]{2,1,0:T(8,128)(2,1)S(1)}, bf16[1,8,25600]{2,1,0:T(8,128)(2,1)S(1)}, u32[]{:S(2)}, u32[]{:S(2)}) collective-permute-start(bf16[1,8,25600]{2,1,0:T(8,128)(2,1)S(1)} %collective-permute-done.4), channel_id=1, source_target_pairs={{0,4},{4,8},{8,12},{12,16},{16,20},{20,24},{24,28},{28,0},{1,5},{5... | collective-permute-start | bytes 1228808 | tf_op jit(solution)/shard_map/ppermute | solution.py:24
  110.1 254.7 %copy-start.15 = (bf16[196,960]{0,1:T(8,128)(2,1)}, bf16[196,960]{0,1:T(8,128)(2,1)S(1)}, u32[]{:S(2)}) copy-start(bf16[196,960]{0,1:T(8,128)(2,1)S(1)} %copy.93) | copy-start | bytes 1128964
  136.3 103.5 %all-gather.2.cloned.1.call-start = ((), (), s32[]{:S(2)}) async-start(), calls=%async_computation.3 | async-start | bytes 7372800 | tf_op jit(solution)/shard_map/all_gather | solution.py:132
  138.8 218.6 %all-reduce.8.cloned.1.call-start = ((), (), s32[]{:S(2)}) async-start(), calls=%async_computation.4 | async-start | bytes 1024000 | tf_op jit(solution)/shard_map/psum | solution.py:211
  325.8 99.6 %all-reduce.10.cloned.1.call-start = ((), (), s32[]{:S(2)}) async-start(), calls=%async_computation.7 | async-start | bytes 2048000 | tf_op jit(solution)/shard_map/psum | solution.py:190
  388.9 229.5 %reduce-scatter.3.cloned.1.call-start = ((), (), s32[]{:S(2)}) async-start(), calls=%async_computation.5 | async-start | bytes 7372800 | tf_op jit(solution)/shard_map/reduce_scatter | solution.py:291
  393.9 31.5 %copy-start.24 = (bf16[1,196,1280]{2,1,0:T(8,128)(2,1)S(1)}, bf16[1,196,1280]{2,1,0:T(8,128)(2,1)}, u32[]{:S(2)}) copy-start(bf16[1,196,1280]{2,1,0:T(8,128)(2,1)} %param.23) | copy-start | bytes 1505284
  393.9 31.5 %copy-start.38 = (f32[196]{0:T(256)S(1)}, f32[196]{0:T(256)}, u32[]{:S(2)}) copy-start(f32[196]{0:T(256)} %copy-done.37) | copy-start | bytes 2356
  393.9 31.5 %copy-start.40 = (f32[1,196]{1,0:T(1,128)S(1)}, f32[1,196]{1,0:T(1,128)}, u32[]{:S(2)}) copy-start(f32[1,196]{1,0:T(1,128)} %copy-done.39) | copy-start | bytes 2356
  393.9 31.5 %copy-start.45 = (f32[196]{0:T(256)S(1)}, f32[196]{0:T(256)}, u32[]{:S(2)}) copy-start(f32[196]{0:T(256)} %copy-done.44) | copy-start | bytes 2356
  393.9 34.0 %copy-start.7 = (f32[196,1280]{1,0:T(8,128)S(1)}, f32[196,1280]{1,0:T(8,128)}, u32[]{:S(2)}) copy-start(f32[196,1280]{1,0:T(8,128)} %copy-done.6) | copy-start | bytes 3010564
  461.6 340.8 %reduce-scatter.5.cloned.1.call-start = ((), (), s32[]{:S(2)}) async-start(), calls=%async_computation.6 | async-start | bytes 14745600 | tf_op jit(solution)/shard_map/reduce_scatter | solution.py:292
  559.5 17.6 %copy-start.46 = (f32[1280]{0:T(1024)S(1)}, f32[1280]{0:T(1024)}, u32[]{:S(2)}) copy-start(f32[1280]{0:T(1024)} %get-tuple-element.130) | copy-start | bytes 15364
  (45 other events, 228.8 us)
Sparse Core Ops, SparseCore 0:
  136.4 31.8 all-reduce.5
  325.9 31.4 all-reduce.7
  389.1 36.3 all-reduce.9
Sparse Core Ops, SparseCore 1:
  139.6 100.2 all-gather.1
  461.7 122.5 reduce-scatter.2
  588.3 214.0 reduce-scatter.4
